TPU v7x, 32 devices: a whole 2x2x4 slice. The times are simulated.
32 devices in a mesh: dp: 4 (over x, core), wide: 8 (over z, y).
Axes of the slice: x: 2, y: 2, z: 4, core: 2. Of those that a mesh axis runs over, the one named last changes fastest.
Arguments:
- streams: float32 [4, 4096, 2048], P(None, 'dp', 'wide'), may hold values from -8 to 8
- cotangent: float32 [4, 4096, 2048], P(None, 'dp', 'wide'), may hold values from -6 to 6
- w_query: bfloat16 [2048, 2048], P('dp', 'wide'), may hold values from -2 to 2
- w_key: bfloat16 [2048, 2048], P('dp', 'wide'), may hold values from -0.125 to 0.125
- w_value: bfloat16 [2048, 2048], P('dp', 'wide'), may hold values from -0.125 to 0.125
- w_out: bfloat16 [2048, 2048], P('wide', 'dp'), may hold values from -1 to 1
- w_gate: bfloat16 [2048, 8192], P('dp', 'wide'), may hold values from -0.125 to 0.125
- w_up: bfloat16 [2048, 8192], P('dp', 'wide'), may hold values from -0.125 to 0.125
- w_down: bfloat16 [8192, 2048], P('wide', 'dp'), may hold values from -0.0625 to 0.0625
- hyper: float32 [2, 4, 6], replicated, may hold values from 0.1 to 0.6
- doc_ids: int32 [4, 1024], P('dp'), may hold values from 0 to 3, never falling along the last dimension, each value on 1 to 512 neighbouring positions
- span_starts: int32 [4, 2], P('dp'), may hold values from 0 to 768, as said below
- span_lengths: int32 [4, 2], P('dp'), may hold values from 64 to 256
Outputs:
- out_streams: float32 [4, 4096, 2048], P(None, 'dp', 'wide')
- d_streams: float32 [4, 4096, 2048], P(None, 'dp', 'wide')
- grad_query: float32 [2048, 2048], P('dp', 'wide')
- grad_key: float32 [2048, 2048], P('dp', 'wide')
- grad_value: float32 [2048, 2048], P('dp', 'wide')
- grad_out: float32 [2048, 2048], P('wide', 'dp')
- grad_gate: float32 [2048, 8192], P('dp', 'wide')
- grad_up: float32 [2048, 8192], P('dp', 'wide')
- grad_down: float32 [8192, 2048], P('wide', 'dp')
- grad_hyper: float32 [2, 4, 6], replicated
- clip_scale: float32 [16], P('wide')
- query_clipped: float32 [2048, 2048], P('dp', 'wide')
- key_clipped: float32 [2048, 2048], P('dp', 'wide')
Inputs may be any that keep to these rules, and one draw needn't show every extreme that they name: `doc_ids`: each row's document numbers never fall; every document holds 1 to 512 tokens, and one holds exactly 512. `span_starts`: span k of a sequence starts and ends inside the k-th of 2 equal regions of the sequence.
All inputs are finite; a program needn't handle non-finite values.
Results may differ from a plain program's by a relative error of at most 0.018.
Values may be sent and summed in bfloat16 or wider, within the bound.
A program may use at most 192 MiB of HBM per device.

v0:
```python
import math
import jax
import jax.numpy as jnp
from jax import lax
from jax.sharding import PartitionSpec as P

D = 2048
H = 16
CLIP_TAU = 6
EPSILON = 1e-05
MASKED = -1e30


def rope_tables(length, head_size):
    half_size = head_size // 2
    inverse = 10000.0 ** (-2.0 * jnp.arange(half_size, dtype=jnp.float32) / head_size)
    angles = jnp.arange(length, dtype=jnp.float32)[:, None] * inverse[None, :]
    cosine_table = jnp.cos(angles)
    sine_table = jnp.sin(angles)
    return (
        jnp.concatenate([cosine_table, cosine_table], axis=1),
        jnp.concatenate([sine_table, sine_table], axis=1),
    )


def rotate(values, cosine_table, sine_table):
    half_size = values.shape[-1] // 2
    turned = jnp.concatenate([-values[..., half_size:], values[..., :half_size]], axis=-1)
    return values * cosine_table[:, None, :] + turned * sine_table[:, None, :]


def rotate_back(grads, cosine_table, sine_table):
    half_size = grads.shape[-1] // 2
    scaled = grads * sine_table[:, None, :]
    turned = jnp.concatenate([scaled[..., half_size:], -scaled[..., :half_size]], axis=-1)
    return grads * cosine_table[:, None, :] + turned


def mix_inputs(weights_in, stream_set):
    return jnp.sum(weights_in[:, None, None] * stream_set, axis=0)


def mix_streams(matrix, stream_set):
    return jnp.sum(matrix[:, :, None, None] * stream_set[None, :, :, :], axis=1)


def mix_back(matrix, grads):
    return jnp.sum(matrix[:, :, None, None] * grads[:, None, :, :], axis=0)


def hyper_rows(pre_grad, post_grad, mix_grad):
    return jnp.concatenate([pre_grad[:, None], post_grad[:, None], mix_grad], axis=1)


def span_labels(positions, starts, lengths):
    inside = (positions[:, None] >= starts[None, :]) & (
        positions[:, None] < (starts + lengths)[None, :]
    )
    numbers = jnp.arange(1, starts.shape[0] + 1, dtype=jnp.int32)
    return jnp.sum(jnp.where(inside, numbers[None, :], 0), axis=1)


def block_mask(doc_row, labels, start_row, count_rows):
    key_pos = jnp.arange(doc_row.shape[0], dtype=jnp.int32)
    query_pos = start_row + jnp.arange(count_rows, dtype=jnp.int32)
    query_docs = lax.dynamic_slice_in_dim(doc_row, start_row, count_rows)
    query_labels = lax.dynamic_slice_in_dim(labels, start_row, count_rows)
    same_doc = query_docs[:, None] == doc_row[None, :]
    causal = key_pos[None, :] <= query_pos[:, None]
    joint_span = (query_labels[:, None] > 0) & (query_labels[:, None] == labels[None, :])
    return same_doc & (causal | joint_span)


def attend_forward(queries, keys_roped, values, doc_row, starts, lengths, score_scale):
    length, head_count, head_size = queries.shape
    block_rows = min(512, length)
    labels = span_labels(jnp.arange(length, dtype=jnp.int32), starts, lengths)

    def one_block(block_index):
        start_row = block_index * block_rows
        query_rows = lax.dynamic_slice_in_dim(queries, start_row, block_rows, 0)
        scores = (
            jnp.einsum("qhd,khd->hqk", query_rows, keys_roped, preferred_element_type=jnp.float32)
            * score_scale
        )
        allowed = block_mask(doc_row, labels, start_row, block_rows)
        masked = jnp.where(allowed[None, :, :], scores, MASKED)
        largest = jnp.max(masked, axis=2)
        exponent = jnp.exp(masked - largest[:, :, None])
        totals = jnp.sum(exponent, axis=2)
        weights_low = (exponent / totals[:, :, None]).astype(jnp.bfloat16)
        attended = jnp.einsum(
            "hqk,khd->qhd", weights_low, values, preferred_element_type=jnp.float32
        )
        return (attended, largest + jnp.log(totals), jnp.max(largest, axis=1))

    attended, log_sums, block_tops = lax.map(
        one_block, jnp.arange(length // block_rows, dtype=jnp.int32)
    )
    return (attended.reshape(length, head_count, head_size), log_sums, jnp.max(block_tops, axis=0))


def attend_backward(
    queries, keys_roped, values, dout, log_sums, doc_row, starts, lengths, score_scale
):
    length, head_count, head_size = queries.shape
    block_rows = min(512, length)
    labels = span_labels(jnp.arange(length, dtype=jnp.int32), starts, lengths)

    def one_block(carry, inputs):
        key_grad, value_grad = carry
        block_index, log_rows = inputs
        start_row = block_index * block_rows
        query_rows = lax.dynamic_slice_in_dim(queries, start_row, block_rows, 0)
        dout_rows = lax.dynamic_slice_in_dim(dout, start_row, block_rows, 0)
        scores = (
            jnp.einsum("qhd,khd->hqk", query_rows, keys_roped, preferred_element_type=jnp.float32)
            * score_scale
        )
        allowed = block_mask(doc_row, labels, start_row, block_rows)
        masked = jnp.where(allowed[None, :, :], scores, MASKED)
        weights_full = jnp.where(allowed[None, :, :], jnp.exp(masked - log_rows[:, :, None]), 0.0)
        weight_grad = jnp.einsum(
            "qhd,khd->hqk", dout_rows, values, preferred_element_type=jnp.float32
        )
        centre = jnp.sum(weights_full * weight_grad, axis=2, keepdims=True)
        score_grad = (weights_full * (weight_grad - centre)).astype(jnp.bfloat16)
        query_grad = score_scale * jnp.einsum(
            "hqk,khd->qhd", score_grad, keys_roped, preferred_element_type=jnp.float32
        )
        key_grad = key_grad + score_scale * jnp.einsum(
            "hqk,qhd->khd", score_grad, query_rows, preferred_element_type=jnp.float32
        )
        value_grad = value_grad + jnp.einsum(
            "hqk,qhd->khd",
            weights_full.astype(jnp.bfloat16),
            dout_rows,
            preferred_element_type=jnp.float32,
        )
        return ((key_grad, value_grad), query_grad)

    empty_grad = jnp.zeros((length, head_count, head_size), jnp.float32)
    count_blocks = length // block_rows
    (key_grad, value_grad), query_grad = lax.scan(
        one_block, (empty_grad, empty_grad), (jnp.arange(count_blocks, dtype=jnp.int32), log_sums)
    )
    return (query_grad.reshape(length, head_count, head_size), key_grad, value_grad)


def row_sums(first_term, second_term):
    return lax.psum((jnp.sum(first_term, axis=1), jnp.sum(second_term, axis=1)), "wide")


def features(piece):
    return lax.all_gather(piece, "wide", axis=1, tiled=True)


def branch_rows(partial_value):
    return lax.psum_scatter(partial_value, "wide", scatter_dimension=1, tiled=True)


def norm_forward(hidden):
    local_width = hidden.shape[1]
    full_width = local_width * lax.axis_size("wide")
    row_total, squares = row_sums(hidden, hidden * hidden)
    centre = row_total / full_width
    spread = squares / full_width - centre * centre
    inverse = lax.rsqrt(spread + EPSILON)
    normed = (hidden - centre[:, None]) * inverse[:, None]
    return (features(normed.astype(jnp.bfloat16)), normed, inverse)


def norm_backward(partial_value, normed, inverse):
    full_width = partial_value.shape[1]
    grad_rows = lax.psum_scatter(partial_value, "wide", scatter_dimension=1, tiled=True)
    row_total, row_cross = row_sums(grad_rows, grad_rows * normed)
    return inverse[:, None] * (
        grad_rows - row_total[:, None] / full_width - normed * row_cross[:, None] / full_width
    )


def per_device(
    streams,
    cotangent,
    w_query,
    w_key,
    w_value,
    w_out,
    w_gate,
    w_up,
    w_down,
    hyper,
    doc_ids,
    span_starts,
    span_lengths,
):
    seq_count, length = doc_ids.shape
    tokens = streams.shape[1]
    head_size = D // H
    column_count = w_query.shape[1]
    head_count = column_count // head_size
    score_scale = 1.0 / math.sqrt(head_size)
    cosine_table, sine_table = rope_tables(length, head_size)
    shape_heads = (seq_count, length, head_count, head_size)
    attn_pre, attn_post, attn_mix = (hyper[0, :, 0], hyper[0, :, 1], hyper[0, :, 2:])
    ffn_pre, ffn_post, ffn_mix = (hyper[1, :, 0], hyper[1, :, 1], hyper[1, :, 2:])
    query_w, key_w, value_w, out_w = (
        lax.all_gather(w_query, "dp", axis=0, tiled=True),
        lax.all_gather(w_key, "dp", axis=0, tiled=True),
        lax.all_gather(w_value, "dp", axis=0, tiled=True),
        lax.all_gather(w_out, "dp", axis=1, tiled=True),
    )
    gate_w, up_w, down_w = (
        lax.all_gather(w_gate, "dp", axis=0, tiled=True),
        lax.all_gather(w_up, "dp", axis=0, tiled=True),
        lax.all_gather(w_down, "dp", axis=1, tiled=True),
    )
    normed_one, kept_one, inverse_one = norm_forward(mix_inputs(attn_pre, streams))
    query_raw = jnp.dot(normed_one, query_w, preferred_element_type=jnp.float32).reshape(
        shape_heads
    )
    key_raw = jnp.dot(normed_one, key_w, preferred_element_type=jnp.float32).reshape(shape_heads)
    values = (
        jnp.dot(normed_one, value_w, preferred_element_type=jnp.float32)
        .astype(jnp.bfloat16)
        .reshape(shape_heads)
    )
    queries = rotate(query_raw, cosine_table, sine_table).astype(jnp.bfloat16)
    keys_roped = rotate(key_raw, cosine_table, sine_table).astype(jnp.bfloat16)

    def forward_sequence(inputs):
        return attend_forward(
            inputs[0], inputs[1], inputs[2], inputs[3], inputs[4], inputs[5], score_scale
        )

    attended, log_sums, seq_tops = lax.map(
        forward_sequence, (queries, keys_roped, values, doc_ids, span_starts, span_lengths)
    )
    head_top = lax.pmax(jnp.max(seq_tops, axis=0), "dp")
    attended_low = attended.reshape(tokens, column_count).astype(jnp.bfloat16)
    branch_one = branch_rows(jnp.dot(attended_low, out_w, preferred_element_type=jnp.float32))
    after_attn = mix_streams(attn_mix, streams) + attn_post[:, None, None] * branch_one[None, :, :]
    normed_two, kept_two, inverse_two = norm_forward(mix_inputs(ffn_pre, after_attn))
    gate_proj = jnp.dot(normed_two, gate_w, preferred_element_type=jnp.float32)
    up_proj = jnp.dot(normed_two, up_w, preferred_element_type=jnp.float32)
    sigmoid_gate = jax.nn.sigmoid(gate_proj)
    hidden = (gate_proj * sigmoid_gate * up_proj).astype(jnp.bfloat16)
    branch_two = branch_rows(jnp.dot(hidden, down_w, preferred_element_type=jnp.float32))
    out_streams = (
        mix_streams(ffn_mix, after_attn) + ffn_post[:, None, None] * branch_two[None, :, :]
    )
    ffn_post_grad = jnp.sum(cotangent * branch_two[None, :, :], axis=(1, 2))
    ffn_mix_grad = jnp.sum(cotangent[:, None, :, :] * after_attn[None, :, :, :], axis=(2, 3))
    two_grad = features(jnp.sum(ffn_post[:, None, None] * cotangent, axis=0).astype(jnp.bfloat16))
    hidden_grad = jnp.dot(two_grad, down_w.T, preferred_element_type=jnp.float32)
    down_wgrad = jnp.einsum("tf,td->fd", hidden, two_grad, preferred_element_type=jnp.float32)
    gate_grad = (
        hidden_grad * up_proj * sigmoid_gate * (1.0 + gate_proj * (1.0 - sigmoid_gate))
    ).astype(jnp.bfloat16)
    up_grad = (hidden_grad * gate_proj * sigmoid_gate).astype(jnp.bfloat16)
    gate_wgrad = jnp.einsum("td,tf->df", normed_two, gate_grad, preferred_element_type=jnp.float32)
    up_wgrad = jnp.einsum("td,tf->df", normed_two, up_grad, preferred_element_type=jnp.float32)
    gate_shard, up_shard, down_shard = (
        lax.psum_scatter(gate_wgrad, "dp", scatter_dimension=0, tiled=True),
        lax.psum_scatter(up_wgrad, "dp", scatter_dimension=0, tiled=True),
        lax.psum_scatter(down_wgrad, "dp", scatter_dimension=1, tiled=True),
    )
    normed_two_grad = jnp.dot(gate_grad, gate_w.T, preferred_element_type=jnp.float32) + jnp.dot(
        up_grad, up_w.T, preferred_element_type=jnp.float32
    )
    h_two_grad = norm_backward(normed_two_grad, kept_two, inverse_two)
    ffn_pre_grad = jnp.sum(h_two_grad[None, :, :] * after_attn, axis=(1, 2))
    after_grad = mix_back(ffn_mix, cotangent) + ffn_pre[:, None, None] * h_two_grad[None, :, :]
    attn_post_grad = jnp.sum(after_grad * branch_one[None, :, :], axis=(1, 2))
    attn_mix_grad = jnp.sum(after_grad[:, None, :, :] * streams[None, :, :, :], axis=(2, 3))
    one_grad = features(jnp.sum(attn_post[:, None, None] * after_grad, axis=0).astype(jnp.bfloat16))
    attended_grad = jnp.dot(one_grad, out_w.T, preferred_element_type=jnp.float32).astype(
        jnp.bfloat16
    )
    out_wgrad = jnp.einsum("tc,td->cd", attended_low, one_grad, preferred_element_type=jnp.float32)

    def backward_sequence(inputs):
        return attend_backward(
            inputs[0],
            inputs[1],
            inputs[2],
            inputs[3],
            inputs[4],
            inputs[5],
            inputs[6],
            inputs[7],
            score_scale,
        )

    query_grad, key_grad, value_grad = lax.map(
        backward_sequence,
        (
            queries,
            keys_roped,
            values,
            attended_grad.reshape(shape_heads),
            log_sums,
            doc_ids,
            span_starts,
            span_lengths,
        ),
    )
    query_low = (
        rotate_back(query_grad, cosine_table, sine_table)
        .reshape(tokens, column_count)
        .astype(jnp.bfloat16)
    )
    key_low = (
        rotate_back(key_grad, cosine_table, sine_table)
        .reshape(tokens, column_count)
        .astype(jnp.bfloat16)
    )
    value_low = value_grad.reshape(tokens, column_count).astype(jnp.bfloat16)
    query_wgrad = jnp.einsum("td,tc->dc", normed_one, query_low, preferred_element_type=jnp.float32)
    key_wgrad = jnp.einsum("td,tc->dc", normed_one, key_low, preferred_element_type=jnp.float32)
    value_wgrad = jnp.einsum("td,tc->dc", normed_one, value_low, preferred_element_type=jnp.float32)
    normed_one_grad = (
        jnp.dot(query_low, query_w.T, preferred_element_type=jnp.float32)
        + jnp.dot(key_low, key_w.T, preferred_element_type=jnp.float32)
        + jnp.dot(value_low, value_w.T, preferred_element_type=jnp.float32)
    )
    h_one_grad = norm_backward(normed_one_grad, kept_one, inverse_one)
    attn_pre_grad = jnp.sum(h_one_grad[None, :, :] * streams, axis=(1, 2))
    streams_grad = mix_back(attn_mix, after_grad) + attn_pre[:, None, None] * h_one_grad[None, :, :]
    hyper_grad = lax.psum(
        jnp.stack(
            [
                hyper_rows(attn_pre_grad, attn_post_grad, attn_mix_grad),
                hyper_rows(ffn_pre_grad, ffn_post_grad, ffn_mix_grad),
            ]
        ),
        ("dp", "wide"),
    )
    query_shard, key_shard, value_shard, out_shard = (
        lax.psum_scatter(query_wgrad, "dp", scatter_dimension=0, tiled=True),
        lax.psum_scatter(key_wgrad, "dp", scatter_dimension=0, tiled=True),
        lax.psum_scatter(value_wgrad, "dp", scatter_dimension=0, tiled=True),
        lax.psum_scatter(out_wgrad, "dp", scatter_dimension=1, tiled=True),
    )
    clip_scale = jnp.sqrt(CLIP_TAU / jnp.maximum(head_top, CLIP_TAU))
    columns = jnp.repeat(clip_scale, head_size)[None, :]
    return (
        out_streams,
        streams_grad,
        query_shard,
        key_shard,
        value_shard,
        out_shard,
        gate_shard,
        up_shard,
        down_shard,
        hyper_grad,
        clip_scale,
        w_query.astype(jnp.float32) * columns,
        w_key.astype(jnp.float32) * columns,
    )


def solution(mesh):
    return jax.shard_map(
        per_device,
        mesh=mesh,
        in_specs=(
            P(None, "dp", "wide"),
            P(None, "dp", "wide"),
            P("dp", "wide"),
            P("dp", "wide"),
            P("dp", "wide"),
            P("wide", "dp"),
            P("dp", "wide"),
            P("dp", "wide"),
            P("wide", "dp"),
            P(),
            P("dp", None),
            P("dp", None),
            P("dp", None),
        ),
        out_specs=(
            P(None, "dp", "wide"),
            P(None, "dp", "wide"),
            P("dp", "wide"),
            P("dp", "wide"),
            P("dp", "wide"),
            P("wide", "dp"),
            P("dp", "wide"),
            P("dp", "wide"),
            P("wide", "dp"),
            P(),
            P("wide"),
            P("dp", "wide"),
            P("dp", "wide"),
        ),
        check_vma=False,
    )
```

profile of v0, /device:TPU:0, one launch (start us, length us, event | category | flops | bytes accessed | tf_op | source)
XLA Modules:
  0.0 1579.7 jit_solution(8456090871075567823)
XLA Ops:
  11.9 23.4 %all-reduce.3 = (f32[1024]{0:T(1024)S(1)}, f32[1024]{0:T(1024)S(1)}) all-reduce(f32[1024]{0:T(1024)S(1)} %multiply_reduce_fusion.20, f32[1024]{0:T(1024)S(1)} %get-tuple-element.312), channel_id=1, replica_groups=mesh['dp'=4,'wide'=8] {'wide'}, use_global_device_ids=true, to_apply=%region_5.6 | all-reduce | flops 2048 | bytes 16384 | tf_op jit(solution)/shard_map/psum | solution.py:151
  42.8 66.4 %all-gather.12.cloned.1.call-done = bf16[1024,2048]{1,0:T(8,128)(2,1)} async-done(((bf16[1024,256]{1,0:T(8,128)(2,1)}), bf16[1024,2048]{1,0:T(8,128)(2,1)}) %all-gather.12.cloned.1.call-update) | async-done | bytes 4194320 | tf_op jit(solution)/shard_map/all_gather | solution.py:155
  147.9 14.2 while.53
  175.5 141.2 %reduce-scatter.12.cloned.1.call-done = f32[1024,256]{1,0:T(8,128)} async-done(((f32[1024,2048]{1,0:T(8,128)}), f32[1024,256]{1,0:T(8,128)}) %reduce-scatter.12.cloned.1.call-update) | async-done | bytes 1048592 | tf_op jit(solution)/shard_map/reduce_scatter | solution.py:159
  322.2 19.7 %all-reduce.2 = (f32[1024]{0:T(1024)S(1)}, f32[1024]{0:T(1024)S(1)}) all-reduce(f32[1024]{0:T(1024)S(1)} %multiply_reduce_fusion.19, f32[1024]{0:T(1024)S(1)} %get-tuple-element.310), channel_id=1, replica_groups=mesh['dp'=4,'wide'=8] {'wide'}, use_global_device_ids=true, to_apply=%region_18.19 | all-reduce | flops 2048 | bytes 16384 | tf_op jit(solution)/shard_map/psum | solution.py:151
  351.8 77.3 %all-gather.22.cloned.1.call-done = bf16[1024,2048]{1,0:T(8,128)(2,1)} async-done(((bf16[1024,256]{1,0:T(8,128)(2,1)}), bf16[1024,2048]{1,0:T(8,128)(2,1)}) %all-gather.22.cloned.1.call-update) | async-done | bytes 4194320 | tf_op jit(solution)/shard_map/all_gather | solution.py:155
  439.1 24.3 %all-gather.26.cloned.1.call-done = bf16[2048,1024]{1,0:T(8,128)(2,1)} async-done(((bf16[512,1024]{1,0:T(8,128)(2,1)}), bf16[2048,1024]{1,0:T(8,128)(2,1)}) %all-gather.26.cloned.1.call-update) | async-done | bytes 4194320 | tf_op jit(solution)/shard_map/all_gather | solution.py:215
  475.4 23.8 %all-gather.28.cloned.1.call-done = bf16[1024,2048]{1,0:T(8,128)(2,1)} async-done(((bf16[1024,512]{1,0:T(8,128)(2,1)}), bf16[1024,2048]{1,0:T(8,128)(2,1)}) %all-gather.28.cloned.1.call-update) | async-done | bytes 4194320 | tf_op jit(solution)/shard_map/all_gather | solution.py:216
  520.7 137.2 %reduce-scatter.14.cloned.1.call-done = f32[1024,256]{1,0:T(8,128)} async-done(((f32[1024,2048]{1,0:T(8,128)}), f32[1024,256]{1,0:T(8,128)}) %reduce-scatter.14.cloned.1.call-update) | async-done | bytes 1048592 | tf_op jit(solution)/shard_map/reduce_scatter | solution.py:159
  666.3 73.4 %all-gather.30.cloned.1.call-done = bf16[1024,2048]{1,0:T(8,128)(2,1)} async-done(((bf16[1024,256]{1,0:T(8,128)(2,1)}), bf16[1024,2048]{1,0:T(8,128)(2,1)}) %all-gather.30.cloned.1.call-update) | async-done | bytes 4194320 | tf_op jit(solution)/shard_map/all_gather | solution.py:155
  739.7 12.9 multiply_convert_fusion.1
  766.6 146.1 %reduce-scatter.16.cloned.1.call-done = f32[1024,256]{1,0:T(8,128)} async-done(((f32[1024,2048]{1,0:T(8,128)}), f32[1024,256]{1,0:T(8,128)}) %reduce-scatter.16.cloned.1.call-update) | async-done | bytes 1048592 | tf_op jit(solution)/shard_map/reduce_scatter | solution.py:175
  914.6 19.9 %all-reduce.1 = (f32[1024]{0:T(1024)S(1)}, f32[1024]{0:T(1024)S(1)}) all-reduce(f32[1024]{0:T(1024)S(1)} %get-tuple-element.326, f32[1024]{0:T(1024)S(1)} %get-tuple-element.325), channel_id=1, replica_groups=mesh['dp'=4,'wide'=8] {'wide'}, use_global_device_ids=true, to_apply=%region_26.27 | all-reduce | flops 2048 | bytes 16384 | tf_op jit(solution)/shard_map/psum | solution.py:151
  948.7 68.3 %all-gather.32.cloned.1.call-done = bf16[1024,2048]{1,0:T(8,128)(2,1)} async-done(((bf16[1024,256]{1,0:T(8,128)(2,1)}), bf16[1024,2048]{1,0:T(8,128)(2,1)}) %all-gather.32.cloned.1.call-update) | async-done | bytes 4194320 | tf_op jit(solution)/shard_map/all_gather | solution.py:155
  1020.7 30.5 %while.54 = (s32[]{:T(128)}, f32[1024,2,128]{0,2,1:T(8,128)S(1)}, f32[1024,2,128]{0,2,1:T(8,128)}, f32[2,512,2,128]{3,1,2,0:T(8,128)}, s32[2]{0:T(128)S(1)}, /*i...) while((s32[]{:T(128)}, f32[1024,2,128]{0,2,1:T(8,128)S(1)}, ...), condition=%wide.region_31.32_spmd.clone.clone, body=%wide.region_29.31_spmd.clone.sunk.clone | while | flops 1357250560 | bytes 90224648 | solution.py:144
  1135.9 76.0 %reduce-scatter.18.cloned.1.call-done = f32[1024,256]{1,0:T(8,128)} async-done(((f32[1024,2048]{1,0:T(8,128)}), f32[1024,256]{1,0:T(8,128)}) %reduce-scatter.18.cloned.1.call-update) | async-done | bytes 1048592 | tf_op jit(solution)/shard_map/reduce_scatter | solution.py:175
  1213.8 19.7 %all-reduce = (f32[1024]{0:T(1024)S(1)}, f32[1024]{0:T(1024)S(1)}) all-reduce(f32[1024]{0:T(1024)S(1)} %get-tuple-element.324, f32[1024]{0:T(1024)S(1)} %get-tuple-element.323), channel_id=1, replica_groups=mesh['dp'=4,'wide'=8] {'wide'}, use_global_device_ids=true, to_apply=%region_36.37 | all-reduce | flops 2048 | bytes 16384 | tf_op jit(solution)/shard_map/psum | solution.py:151
  1242.9 38.0 %psum.71 = f32[2,4,6]{2,1,0:T(4,128)} all-reduce(f32[2,4,6]{2,1,0:T(4,128)S(1)} %pad_maximum_fusion.3), channel_id=1, replica_groups=mesh['dp'=4,'wide'=8] {'dp','wide'}, use_global_device_ids=true, to_apply=%region_50.51 | all-reduce | flops 48 | bytes 384 | tf_op jit(solution)/shard_map/psum | solution.py:330
  1286.7 74.4 %reduce-scatter.28.cloned.1.call-done = f32[512,1024]{1,0:T(8,128)} async-done(((f32[2048,1024]{1,0:T(8,128)}), f32[512,1024]{1,0:T(8,128)}) %reduce-scatter.28.cloned.1.call-update) | async-done | bytes 2097168 | tf_op jit(solution)/shard_map/reduce_scatter | solution.py:264
  1361.1 74.4 %reduce-scatter.30.cloned.1.call-done = f32[512,1024]{1,0:T(8,128)} async-done(((f32[2048,1024]{1,0:T(8,128)}), f32[512,1024]{1,0:T(8,128)}) %reduce-scatter.30.cloned.1.call-update) | async-done | bytes 2097168 | tf_op jit(solution)/shard_map/reduce_scatter | solution.py:265
  1435.6 34.3 %reduce-scatter.22.cloned.1.call-done = f32[512,256]{1,0:T(8,128)} async-done(((f32[2048,256]{1,0:T(8,128)}), f32[512,256]{1,0:T(8,128)}) %reduce-scatter.22.cloned.1.call-update) | async-done | bytes 524304 | tf_op jit(solution)/shard_map/reduce_scatter | solution.py:341
  1469.9 34.2 %reduce-scatter.20.cloned.1.call-done = f32[512,256]{1,0:T(8,128)} async-done(((f32[2048,256]{1,0:T(8,128)}), f32[512,256]{1,0:T(8,128)}) %reduce-scatter.20.cloned.1.call-update) | async-done | bytes 524304 | tf_op jit(solution)/shard_map/reduce_scatter | solution.py:340
  1504.0 34.3 %reduce-scatter.26.cloned.1.call-done = f32[256,512]{1,0:T(8,128)} async-done(((f32[256,2048]{1,0:T(8,128)}), f32[256,512]{1,0:T(8,128)}) %reduce-scatter.26.cloned.1.call-update) | async-done | bytes 524304 | tf_op jit(solution)/shard_map/reduce_scatter | solution.py:343
  1538.4 34.3 %reduce-scatter.24.cloned.1.call-done = f32[512,256]{1,0:T(8,128)} async-done(((f32[2048,256]{1,0:T(8,128)}), f32[512,256]{1,0:T(8,128)}) %reduce-scatter.24.cloned.1.call-update) | async-done | bytes 524304 | tf_op jit(solution)/shard_map/reduce_scatter | solution.py:342
  (302 shorter events, 307.1 us)
Async XLA Ops:
  7.2 35.6 %all-gather.16.cloned.1.call-start = ((), (), s32[]{:S(2)}) async-start(), calls=%async_computation.13 | async-start | bytes 1310720 | tf_op jit(solution)/shard_map/all_gather | solution.py:209
  7.9 101.3 %all-gather.12.cloned.1.call-start = ((), (), s32[]{:S(2)}) async-start(), calls=%async_computation.11 | async-start | bytes 4718592 | tf_op jit(solution)/shard_map/all_gather | solution.py:155
  37.1 88.5 %all-gather.14.cloned.1.call-start = ((), (), s32[]{:S(2)}) async-start(), calls=%async_computation.12 | async-start | bytes 1310720 | tf_op jit(solution)/shard_map/all_gather | solution.py:208
  37.9 105.9 %all-gather.18.cloned.1.call-start = ((), (), s32[]{:S(2)}) async-start(), calls=%async_computation.14 | async-start | bytes 1310720 | tf_op jit(solution)/shard_map/all_gather | solution.py:210
  38.5 124.3 %all-gather.20.cloned.1.call-start = ((), (), s32[]{:S(2)}) async-start(), calls=%async_computation.15 | async-start | bytes 1310720 | tf_op jit(solution)/shard_map/all_gather | solution.py:211
  39.0 277.6 %reduce-scatter.12.cloned.1.call-start = ((), (), s32[]{:S(2)}) async-start(), calls=%async_computation.16 | async-start | bytes 9437184 | tf_op jit(solution)/shard_map/reduce_scatter | solution.py:159
  42.5 902.6 %copy-start.12 = (f32[1024,128]{0,1:T(8,128)}, f32[1024,128]{0,1:T(8,128)S(1)}, u32[]{:S(2)}) copy-start(f32[1024,128]{0,1:T(8,128)S(1)} %copy.61) | copy-start | bytes 1572868
  168.6 183.2 %all-gather.24.cloned.1.call-start = ((), (), s32[]{:S(2)}) async-start(), calls=%async_computation.18 | async-start | bytes 5242880 | tf_op jit(solution)/shard_map/all_gather | solution.py:214
  169.4 259.7 %all-gather.22.cloned.1.call-start = ((), (), s32[]{:S(2)}) async-start(), calls=%async_computation.17 | async-start | bytes 4718592 | tf_op jit(solution)/shard_map/all_gather | solution.py:155
  343.1 120.2 %all-gather.26.cloned.1.call-start = ((), (), s32[]{:S(2)}) async-start(), calls=%async_computation.19 | async-start | bytes 5242880 | tf_op jit(solution)/shard_map/all_gather | solution.py:215
  343.8 155.4 %all-gather.28.cloned.1.call-start = ((), (), s32[]{:S(2)}) async-start(), calls=%async_computation.20 | async-start | bytes 5242880 | tf_op jit(solution)/shard_map/all_gather | solution.py:216
  344.4 313.4 %reduce-scatter.14.cloned.1.call-start = ((), (), s32[]{:S(2)}) async-start(), calls=%async_computation.21 | async-start | bytes 9437184 | tf_op jit(solution)/shard_map/reduce_scatter | solution.py:159
  509.8 229.9 %all-gather.30.cloned.1.call-start = ((), (), s32[]{:S(2)}) async-start(), calls=%async_computation.22 | async-start | bytes 4718592 | tf_op jit(solution)/shard_map/all_gather | solution.py:155
  665.9 246.9 %reduce-scatter.16.cloned.1.call-start = ((), (), s32[]{:S(2)}) async-start(), calls=%async_computation.23 | async-start | bytes 9437184 | tf_op jit(solution)/shard_map/reduce_scatter | solution.py:175
  766.6 250.4 %all-gather.32.cloned.1.call-start = ((), (), s32[]{:S(2)}) async-start(), calls=%async_computation.24 | async-start | bytes 4718592 | tf_op jit(solution)/shard_map/all_gather | solution.py:155
  944.9 267.0 %reduce-scatter.18.cloned.1.call-start = ((), (), s32[]{:S(2)}) async-start(), calls=%async_computation.25 | async-start | bytes 9437184 | tf_op jit(solution)/shard_map/reduce_scatter | solution.py:175
  1065.7 221.0 %reduce-scatter.32.cloned.1.call-start = ((), (), s32[]{:S(2)}) async-start(), calls=%async_computation.32 | async-start | bytes 10485760 | tf_op jit(solution)/shard_map/reduce_scatter | solution.py:266
  1076.6 284.5 %reduce-scatter.28.cloned.1.call-start = ((), (), s32[]{:S(2)}) async-start(), calls=%async_computation.30 | async-start | bytes 10485760 | tf_op jit(solution)/shard_map/reduce_scatter | solution.py:264
  1087.4 348.2 %reduce-scatter.30.cloned.1.call-start = ((), (), s32[]{:S(2)}) async-start(), calls=%async_computation.31 | async-start | bytes 10485760 | tf_op jit(solution)/shard_map/reduce_scatter | solution.py:265
  1098.6 371.3 %reduce-scatter.22.cloned.1.call-start = ((), (), s32[]{:S(2)}) async-start(), calls=%async_computation.27 | async-start | bytes 2621440 | tf_op jit(solution)/shard_map/reduce_scatter | solution.py:341
  1103.5 400.5 %reduce-scatter.20.cloned.1.call-start = ((), (), s32[]{:S(2)}) async-start(), calls=%async_computation.26 | async-start | bytes 2621440 | tf_op jit(solution)/shard_map/reduce_scatter | solution.py:340
  1108.6 429.7 %reduce-scatter.26.cloned.1.call-start = ((), (), s32[]{:S(2)}) async-start(), calls=%async_computation.29 | async-start | bytes 2621440 | tf_op jit(solution)/shard_map/reduce_scatter | solution.py:343
  1113.9 458.8 %reduce-scatter.24.cloned.1.call-start = ((), (), s32[]{:S(2)}) async-start(), calls=%async_computation.28 | async-start | bytes 2621440 | tf_op jit(solution)/shard_map/reduce_scatter | solution.py:342
  1135.9 99.5 %copy-start.39 = (f32[4]{0:T(128)S(1)}, f32[4]{0:T(128)}, u32[]{:S(2)}) copy-start(f32[4]{0:T(128)} %copy-done.38) | copy-start | bytes 52
  (57 other events, 722.8 us)
Sparse Core Ops, SparseCore 0:
  9.5 19.4 all-gather.15
  37.3 71.8 all-gather.11
  110.8 14.8 all-gather.13
  127.1 16.6 all-gather.17
  145.2 16.6 all-gather.19
  168.7 147.8 reduce-scatter.11
  318.2 33.5 all-gather.23
  354.4 74.6 all-gather.21
  430.7 32.6 all-gather.25
  464.7 34.4 all-gather.27
  509.9 147.8 reduce-scatter.13
  666.0 73.7 all-gather.29
  766.7 146.0 reduce-scatter.15
  945.1 71.8 all-gather.31
  1065.9 146.0 reduce-scatter.17
  1214.9 71.7 reduce-scatter.31
  1289.7 71.3 reduce-scatter.27
  1364.1 71.3 reduce-scatter.29
  1438.7 31.1 reduce-scatter.21
  1472.8 31.1 reduce-scatter.19
  1507.2 31.1 reduce-scatter.25
  1541.5 31.1 reduce-scatter.23
where the time goes:
time: 1590 us; the launch traced here: 1580 us
  waiting for transfers between devices  1160 us (73%)
  matrix products  165 us (10%)
  blocking collectives  127 us (8%)
  other arithmetic  86.2 us (5%)
  local copies, waits for them, and re-layouts  21 us (1%)
    all_gather x4, waiting for transfers between devices, features(): return lax.all_gather(piece, 'wide', axis=1, tiled=True)  285 us
    reduce_scatter x2, waiting for transfers between devices, branch_rows(): lax.psum_scatter(partial_value, 'wide', scatter_dimension=1, tiled=True)  278 us
    reduce_scatter x2, waiting for transfers between devices, norm_backward(): lax.psum_scatter(partial_value, 'wide', scatter_dimension=1, tiled=True)  222 us
    psum x4, blocking collectives, row_sums(): lax.psum((jnp.sum(first_term, axis=1), jnp.sum(second_term, axis=1)), 'wi...  82.8 us
    reduce_scatter x1, waiting for transfers between devices, per_device(): lax.psum_scatter(up_wgrad, 'dp', scatter_dimension=0, tiled=True)  74.4 us
    reduce_scatter x1, waiting for transfers between devices, per_device(): lax.psum_scatter(gate_wgrad, 'dp', scatter_dimension=0, tiled=True)  74.4 us
    psum x1, blocking collectives, per_device(): lax.psum(jnp.stack([hyper_rows(attn_pre_grad, attn_post_grad, attn_mix_gr...  38 us
    reduce_scatter x1, waiting for transfers between devices, per_device(): lax.psum_scatter(out_wgrad, 'dp', scatter_dimension=1, tiled=True)  34.3 us
  transfers between devices with their start and end apart: 22, of which 20 were waited for; matrix products, arithmetic and copies ran while one was open for 10% of the time, Pallas kernels for 0%

commit v1 on v0

--- a/solution.py
+++ b/solution.py
@@ -327,14 +327,17 @@
     h_one_grad = norm_backward(normed_one_grad, kept_one, inverse_one)
     attn_pre_grad = jnp.sum(h_one_grad[None, :, :] * streams, axis=(1, 2))
     streams_grad = mix_back(attn_mix, after_grad) + attn_pre[:, None, None] * h_one_grad[None, :, :]
-    hyper_grad = lax.psum(
-        jnp.stack(
-            [
-                hyper_rows(attn_pre_grad, attn_post_grad, attn_mix_grad),
-                hyper_rows(ffn_pre_grad, ffn_post_grad, ffn_mix_grad),
-            ]
+    hyper_grad = jnp.sum(
+        lax.all_gather(
+            jnp.stack(
+                [
+                    hyper_rows(attn_pre_grad, attn_post_grad, attn_mix_grad),
+                    hyper_rows(ffn_pre_grad, ffn_post_grad, ffn_mix_grad),
+                ]
+            ),
+            ("dp", "wide"),
         ),
-        ("dp", "wide"),
+        axis=0,
     )
     query_shard, key_shard, value_shard, out_shard = (
         lax.psum_scatter(query_wgrad, "dp", scatter_dimension=0, tiled=True),

time: 1590 us -> 1590 us (level)
  waiting for transfers between devices: 1160 us -> 1130 us
  blocking collectives: 127 us -> 154 us
    all_gather x0 -> x1, blocking collectives: none -> 65 us  [per_device(): lax.all_gather(jnp.stack([hyper_rows(attn_pre_grad, attn_post_grad, attn_...]
    psum x1 -> x0, blocking collectives: 38 us -> none  [per_device(): lax.psum(jnp.stack([hyper_rows(attn_pre_grad, attn_post_grad, attn_mix_gr...]
    reduce_scatter x1, waiting for transfers between devices: 74.4 us -> 51.2 us  [per_device(): lax.psum_scatter(gate_wgrad, 'dp', scatter_dimension=0, tiled=True)]
  transfers between devices with their start and end apart: 22 -> 22, of which waited for: 20 -> 19; matrix products, arithmetic and copies ran while one was open for 10% -> 10% of each run, Pallas kernels for 0% -> 0%
where the time goes in v1:
time: 1590 us; the launch traced here: 1580 us
  waiting for transfers between devices  1130 us (71%)
  matrix products  165 us (10%)
  blocking collectives  154 us (10%)
  other arithmetic  86.8 us (5%)
  local copies, waits for them, and re-layouts  21 us (1%)
    all_gather x4, waiting for transfers between devices, features(): return lax.all_gather(piece, 'wide', axis=1, tiled=True)  285 us
    reduce_scatter x2, waiting for transfers between devices, branch_rows(): lax.psum_scatter(partial_value, 'wide', scatter_dimension=1, tiled=True)  278 us
    reduce_scatter x2, waiting for transfers between devices, norm_backward(): lax.psum_scatter(partial_value, 'wide', scatter_dimension=1, tiled=True)  222 us
    psum x4, blocking collectives, row_sums(): lax.psum((jnp.sum(first_term, axis=1), jnp.sum(second_term, axis=1)), 'wi...  82.8 us
    reduce_scatter x1, waiting for transfers between devices, per_device(): lax.psum_scatter(up_wgrad, 'dp', scatter_dimension=0, tiled=True)  74.4 us
    all_gather x1, blocking collectives, per_device(): lax.all_gather(jnp.stack([hyper_rows(attn_pre_grad, attn_post_grad, attn_...  65 us
    reduce_scatter x1, waiting for transfers between devices, per_device(): lax.psum_scatter(gate_wgrad, 'dp', scatter_dimension=0, tiled=True)  51.2 us
    reduce_scatter x1, waiting for transfers between devices, per_device(): lax.psum_scatter(out_wgrad, 'dp', scatter_dimension=1, tiled=True)  34.3 us
  transfers between devices with their start and end apart: 22, of which 19 were waited for; matrix products, arithmetic and copies ran while one was open for 10% of the time, Pallas kernels for 0%

profile of v1, /device:TPU:0, one launch (start us, length us, event | category | flops | bytes accessed | tf_op | source)
XLA Modules:
  0.0 1578.3 jit_solution(4935239182831670344)
XLA Ops:
  11.9 23.4 %all-reduce.3 = (f32[1024]{0:T(1024)S(1)}, f32[1024]{0:T(1024)S(1)}) all-reduce(f32[1024]{0:T(1024)S(1)} %multiply_reduce_fusion.20, f32[1024]{0:T(1024)S(1)} %get-tuple-element.334), channel_id=1, replica_groups=mesh['dp'=4,'wide'=8] {'wide'}, use_global_device_ids=true, to_apply=%region_5.6 | all-reduce | flops 2048 | bytes 16384 | tf_op jit(solution)/shard_map/psum | solution.py:151
  42.8 66.4 %all-gather.13.cloned.1.call-done = bf16[1024,2048]{1,0:T(8,128)(2,1)} async-done(((bf16[1024,256]{1,0:T(8,128)(2,1)}), bf16[1024,2048]{1,0:T(8,128)(2,1)}) %all-gather.13.cloned.1.call-update) | async-done | bytes 4194320 | tf_op jit(solution)/shard_map/all_gather | solution.py:155
  147.9 14.2 while.53
  175.5 141.2 %reduce-scatter.12.cloned.1.call-done = f32[1024,256]{1,0:T(8,128)} async-done(((f32[1024,2048]{1,0:T(8,128)}), f32[1024,256]{1,0:T(8,128)}) %reduce-scatter.12.cloned.1.call-update) | async-done | bytes 1048592 | tf_op jit(solution)/shard_map/reduce_scatter | solution.py:159
  322.2 19.7 %all-reduce.2 = (f32[1024]{0:T(1024)S(1)}, f32[1024]{0:T(1024)S(1)}) all-reduce(f32[1024]{0:T(1024)S(1)} %multiply_reduce_fusion.19, f32[1024]{0:T(1024)S(1)} %get-tuple-element.332), channel_id=1, replica_groups=mesh['dp'=4,'wide'=8] {'wide'}, use_global_device_ids=true, to_apply=%region_18.19 | all-reduce | flops 2048 | bytes 16384 | tf_op jit(solution)/shard_map/psum | solution.py:151
  351.8 77.3 %all-gather.23.cloned.1.call-done = bf16[1024,2048]{1,0:T(8,128)(2,1)} async-done(((bf16[1024,256]{1,0:T(8,128)(2,1)}), bf16[1024,2048]{1,0:T(8,128)(2,1)}) %all-gather.23.cloned.1.call-update) | async-done | bytes 4194320 | tf_op jit(solution)/shard_map/all_gather | solution.py:155
  439.1 24.3 %all-gather.27.cloned.1.call-done = bf16[2048,1024]{1,0:T(8,128)(2,1)} async-done(((bf16[512,1024]{1,0:T(8,128)(2,1)}), bf16[2048,1024]{1,0:T(8,128)(2,1)}) %all-gather.27.cloned.1.call-update) | async-done | bytes 4194320 | tf_op jit(solution)/shard_map/all_gather | solution.py:215
  475.4 23.8 %all-gather.29.cloned.1.call-done = bf16[1024,2048]{1,0:T(8,128)(2,1)} async-done(((bf16[1024,512]{1,0:T(8,128)(2,1)}), bf16[1024,2048]{1,0:T(8,128)(2,1)}) %all-gather.29.cloned.1.call-update) | async-done | bytes 4194320 | tf_op jit(solution)/shard_map/all_gather | solution.py:216
  520.7 137.2 %reduce-scatter.14.cloned.1.call-done = f32[1024,256]{1,0:T(8,128)} async-done(((f32[1024,2048]{1,0:T(8,128)}), f32[1024,256]{1,0:T(8,128)}) %reduce-scatter.14.cloned.1.call-update) | async-done | bytes 1048592 | tf_op jit(solution)/shard_map/reduce_scatter | solution.py:159
  666.3 73.4 %all-gather.31.cloned.1.call-done = bf16[1024,2048]{1,0:T(8,128)(2,1)} async-done(((bf16[1024,256]{1,0:T(8,128)(2,1)}), bf16[1024,2048]{1,0:T(8,128)(2,1)}) %all-gather.31.cloned.1.call-update) | async-done | bytes 4194320 | tf_op jit(solution)/shard_map/all_gather | solution.py:155
  739.7 12.9 multiply_convert_fusion.1
  766.6 146.1 %reduce-scatter.16.cloned.1.call-done = f32[1024,256]{1,0:T(8,128)} async-done(((f32[1024,2048]{1,0:T(8,128)}), f32[1024,256]{1,0:T(8,128)}) %reduce-scatter.16.cloned.1.call-update) | async-done | bytes 1048592 | tf_op jit(solution)/shard_map/reduce_scatter | solution.py:175
  914.6 19.9 %all-reduce.1 = (f32[1024]{0:T(1024)S(1)}, f32[1024]{0:T(1024)S(1)}) all-reduce(f32[1024]{0:T(1024)S(1)} %get-tuple-element.348, f32[1024]{0:T(1024)S(1)} %get-tuple-element.347), channel_id=1, replica_groups=mesh['dp'=4,'wide'=8] {'wide'}, use_global_device_ids=true, to_apply=%region_26.27 | all-reduce | flops 2048 | bytes 16384 | tf_op jit(solution)/shard_map/psum | solution.py:151
  948.7 68.3 %all-gather.33.cloned.1.call-done = bf16[1024,2048]{1,0:T(8,128)(2,1)} async-done(((bf16[1024,256]{1,0:T(8,128)(2,1)}), bf16[1024,2048]{1,0:T(8,128)(2,1)}) %all-gather.33.cloned.1.call-update) | async-done | bytes 4194320 | tf_op jit(solution)/shard_map/all_gather | solution.py:155
  1020.7 30.5 %while.54 = (s32[]{:T(128)}, f32[1024,2,128]{0,2,1:T(8,128)S(1)}, f32[1024,2,128]{0,2,1:T(8,128)}, f32[2,512,2,128]{3,1,2,0:T(8,128)}, s32[2]{0:T(128)S(1)}, /*i...) while((s32[]{:T(128)}, f32[1024,2,128]{0,2,1:T(8,128)S(1)}, ...), condition=%wide.region_31.32_spmd.clone.clone, body=%wide.region_29.31_spmd.clone.sunk.clone | while | flops 1357250560 | bytes 90224648 | solution.py:144
  1135.9 76.0 %reduce-scatter.18.cloned.1.call-done = f32[1024,256]{1,0:T(8,128)} async-done(((f32[1024,2048]{1,0:T(8,128)}), f32[1024,256]{1,0:T(8,128)}) %reduce-scatter.18.cloned.1.call-update) | async-done | bytes 1048592 | tf_op jit(solution)/shard_map/reduce_scatter | solution.py:175
  1213.8 19.7 %all-reduce = (f32[1024]{0:T(1024)S(1)}, f32[1024]{0:T(1024)S(1)}) all-reduce(f32[1024]{0:T(1024)S(1)} %get-tuple-element.346, f32[1024]{0:T(1024)S(1)} %get-tuple-element.345), channel_id=1, replica_groups=mesh['dp'=4,'wide'=8] {'wide'}, use_global_device_ids=true, to_apply=%region_36.37 | all-reduce | flops 2048 | bytes 16384 | tf_op jit(solution)/shard_map/psum | solution.py:151
  1242.9 65.0 %all-gather = f32[64,4,6]{2,1,0:T(4,128)S(1)} all-gather(f32[2,4,6]{2,1,0:T(4,128)S(1)} %pad_maximum_fusion.3), channel_id=2, replica_groups=mesh['dp'=4,'wide'=8] {'dp','wide'}, dimensions={0}, use_global_device_ids=true | all-gather | bytes 6336 | tf_op jit(solution)/shard_map/all_gather | solution.py:331
  1308.5 51.2 %reduce-scatter.28.cloned.1.call-done = f32[512,1024]{1,0:T(8,128)} async-done(((f32[2048,1024]{1,0:T(8,128)}), f32[512,1024]{1,0:T(8,128)}) %reduce-scatter.28.cloned.1.call-update) | async-done | bytes 2097168 | tf_op jit(solution)/shard_map/reduce_scatter | solution.py:264
  1359.7 74.4 %reduce-scatter.30.cloned.1.call-done = f32[512,1024]{1,0:T(8,128)} async-done(((f32[2048,1024]{1,0:T(8,128)}), f32[512,1024]{1,0:T(8,128)}) %reduce-scatter.30.cloned.1.call-update) | async-done | bytes 2097168 | tf_op jit(solution)/shard_map/reduce_scatter | solution.py:265
  1434.2 34.3 %reduce-scatter.22.cloned.1.call-done = f32[512,256]{1,0:T(8,128)} async-done(((f32[2048,256]{1,0:T(8,128)}), f32[512,256]{1,0:T(8,128)}) %reduce-scatter.22.cloned.1.call-update) | async-done | bytes 524304 | tf_op jit(solution)/shard_map/reduce_scatter | solution.py:344
  1468.5 34.2 %reduce-scatter.20.cloned.1.call-done = f32[512,256]{1,0:T(8,128)} async-done(((f32[2048,256]{1,0:T(8,128)}), f32[512,256]{1,0:T(8,128)}) %reduce-scatter.20.cloned.1.call-update) | async-done | bytes 524304 | tf_op jit(solution)/shard_map/reduce_scatter | solution.py:343
  1502.6 34.3 %reduce-scatter.26.cloned.1.call-done = f32[256,512]{1,0:T(8,128)} async-done(((f32[256,2048]{1,0:T(8,128)}), f32[256,512]{1,0:T(8,128)}) %reduce-scatter.26.cloned.1.call-update) | async-done | bytes 524304 | tf_op jit(solution)/shard_map/reduce_scatter | solution.py:346
  1537.0 34.3 %reduce-scatter.24.cloned.1.call-done = f32[512,256]{1,0:T(8,128)} async-done(((f32[2048,256]{1,0:T(8,128)}), f32[512,256]{1,0:T(8,128)}) %reduce-scatter.24.cloned.1.call-update) | async-done | bytes 524304 | tf_op jit(solution)/shard_map/reduce_scatter | solution.py:345
  (303 shorter events, 302.0 us)
Async XLA Ops:
  7.2 35.6 %all-gather.17.cloned.1.call-start = ((), (), s32[]{:S(2)}) async-start(), calls=%async_computation.13 | async-start | bytes 1310720 | tf_op jit(solution)/shard_map/all_gather | solution.py:209
  7.9 101.3 %all-gather.13.cloned.1.call-start = ((), (), s32[]{:S(2)}) async-start(), calls=%async_computation.11 | async-start | bytes 4718592 | tf_op jit(solution)/shard_map/all_gather | solution.py:155
  37.1 88.5 %all-gather.15.cloned.1.call-start = ((), (), s32[]{:S(2)}) async-start(), calls=%async_computation.12 | async-start | bytes 1310720 | tf_op jit(solution)/shard_map/all_gather | solution.py:208
  37.9 105.9 %all-gather.19.cloned.1.call-start = ((), (), s32[]{:S(2)}) async-start(), calls=%async_computation.14 | async-start | bytes 1310720 | tf_op jit(solution)/shard_map/all_gather | solution.py:210
  38.5 124.3 %all-gather.21.cloned.1.call-start = ((), (), s32[]{:S(2)}) async-start(), calls=%async_computation.15 | async-start | bytes 1310720 | tf_op jit(solution)/shard_map/all_gather | solution.py:211
  39.0 277.6 %reduce-scatter.12.cloned.1.call-start = ((), (), s32[]{:S(2)}) async-start(), calls=%async_computation.16 | async-start | bytes 9437184 | tf_op jit(solution)/shard_map/reduce_scatter | solution.py:159
  42.5 902.6 %copy-start.12 = (f32[1024,128]{0,1:T(8,128)}, f32[1024,128]{0,1:T(8,128)S(1)}, u32[]{:S(2)}) copy-start(f32[1024,128]{0,1:T(8,128)S(1)} %copy.81) | copy-start | bytes 1572868
  168.6 183.2 %all-gather.25.cloned.1.call-start = ((), (), s32[]{:S(2)}) async-start(), calls=%async_computation.18 | async-start | bytes 5242880 | tf_op jit(solution)/shard_map/all_gather | solution.py:214
  169.4 259.7 %all-gather.23.cloned.1.call-start = ((), (), s32[]{:S(2)}) async-start(), calls=%async_computation.17 | async-start | bytes 4718592 | tf_op jit(solution)/shard_map/all_gather | solution.py:155
  343.1 120.2 %all-gather.27.cloned.1.call-start = ((), (), s32[]{:S(2)}) async-start(), calls=%async_computation.19 | async-start | bytes 5242880 | tf_op jit(solution)/shard_map/all_gather | solution.py:215
  343.8 155.4 %all-gather.29.cloned.1.call-start = ((), (), s32[]{:S(2)}) async-start(), calls=%async_computation.20 | async-start | bytes 5242880 | tf_op jit(solution)/shard_map/all_gather | solution.py:216
  344.4 313.4 %reduce-scatter.14.cloned.1.call-start = ((), (), s32[]{:S(2)}) async-start(), calls=%async_computation.21 | async-start | bytes 9437184 | tf_op jit(solution)/shard_map/reduce_scatter | solution.py:159
  509.8 229.9 %all-gather.31.cloned.1.call-start = ((), (), s32[]{:S(2)}) async-start(), calls=%async_computation.22 | async-start | bytes 4718592 | tf_op jit(solution)/shard_map/all_gather | solution.py:155
  665.9 246.9 %reduce-scatter.16.cloned.1.call-start = ((), (), s32[]{:S(2)}) async-start(), calls=%async_computation.23 | async-start | bytes 9437184 | tf_op jit(solution)/shard_map/reduce_scatter | solution.py:175
  766.6 250.4 %all-gather.33.cloned.1.call-start = ((), (), s32[]{:S(2)}) async-start(), calls=%async_computation.24 | async-start | bytes 4718592 | tf_op jit(solution)/shard_map/all_gather | solution.py:155
  944.9 267.0 %reduce-scatter.18.cloned.1.call-start = ((), (), s32[]{:S(2)}) async-start(), calls=%async_computation.25 | async-start | bytes 9437184 | tf_op jit(solution)/shard_map/reduce_scatter | solution.py:175
  1065.7 242.8 %reduce-scatter.32.cloned.1.call-start = ((), (), s32[]{:S(2)}) async-start(), calls=%async_computation.32 | async-start | bytes 10485760 | tf_op jit(solution)/shard_map/reduce_scatter | solution.py:266
  1076.6 283.1 %reduce-scatter.28.cloned.1.call-start = ((), (), s32[]{:S(2)}) async-start(), calls=%async_computation.30 | async-start | bytes 10485760 | tf_op jit(solution)/shard_map/reduce_scatter | solution.py:264
  1087.4 346.8 %reduce-scatter.30.cloned.1.call-start = ((), (), s32[]{:S(2)}) async-start(), calls=%async_computation.31 | async-start | bytes 10485760 | tf_op jit(solution)/shard_map/reduce_scatter | solution.py:265
  1098.6 369.9 %reduce-scatter.22.cloned.1.call-start = ((), (), s32[]{:S(2)}) async-start(), calls=%async_computation.27 | async-start | bytes 2621440 | tf_op jit(solution)/shard_map/reduce_scatter | solution.py:344
  1103.5 399.1 %reduce-scatter.20.cloned.1.call-start = ((), (), s32[]{:S(2)}) async-start(), calls=%async_computation.26 | async-start | bytes 2621440 | tf_op jit(solution)/shard_map/reduce_scatter | solution.py:343
  1108.6 428.3 %reduce-scatter.26.cloned.1.call-start = ((), (), s32[]{:S(2)}) async-start(), calls=%async_computation.29 | async-start | bytes 2621440 | tf_op jit(solution)/shard_map/reduce_scatter | solution.py:346
  1113.9 457.4 %reduce-scatter.24.cloned.1.call-start = ((), (), s32[]{:S(2)}) async-start(), calls=%async_computation.28 | async-start | bytes 2621440 | tf_op jit(solution)/shard_map/reduce_scatter | solution.py:345
  1135.9 99.5 %copy-start.39 = (f32[4]{0:T(128)S(1)}, f32[4]{0:T(128)}, u32[]{:S(2)}) copy-start(f32[4]{0:T(128)} %copy-done.38) | copy-start | bytes 52
  (57 other events, 722.8 us)
Sparse Core Ops, SparseCore 0:
  9.5 19.4 all-gather.16
  37.3 71.8 all-gather.12
  110.8 14.8 all-gather.14
  127.1 16.6 all-gather.18
  145.2 16.6 all-gather.20
  168.7 147.8 reduce-scatter.11
  318.2 33.5 all-gather.24
  354.4 74.6 all-gather.22
  430.7 32.6 all-gather.26
  464.7 34.4 all-gather.28
  509.9 147.8 reduce-scatter.13
  666.0 73.7 all-gather.30
  766.7 146.0 reduce-scatter.15
  945.1 71.8 all-gather.32
  1065.9 146.0 reduce-scatter.17
  1214.9 70.3 reduce-scatter.31
  1288.3 71.3 reduce-scatter.27
  1362.7 71.3 reduce-scatter.29
  1437.3 31.1 reduce-scatter.21
  1471.4 31.1 reduce-scatter.19
  1505.8 31.1 reduce-scatter.25
  1540.1 31.1 reduce-scatter.23
